TPU v7x, 32 devices: a whole 2x2x4 slice. The times are simulated.
32 devices in a mesh: sub: 8 (over z, y), grp: 4 (over x, core).
Axes of the slice: x: 2, y: 2, z: 4, core: 2. Of those that a mesh axis runs over, the one named last changes fastest.
Arguments:
- rr_inverse: float32 [64, 512, 512], P(('sub', 'grp')), may hold values from -4 to 4, as said below
- corner_modes: float32 [64, 64, 512], P(('sub', 'grp')), may hold values from -0.5 to 0.5
- coarse_inverse: float32 [2048, 2048], P(('sub', 'grp')), may hold values from -1 to 1, as said below
- inertia: float32 [64, 512], P(('sub', 'grp')), may hold values from 0.5 to 2
- disp_now: float32 [8, 64, 512], P(None, ('sub', 'grp')), may hold values from -4 to 4
- vel_now: float32 [8, 64, 512], P(None, ('sub', 'grp')), may hold values from -4 to 4
- acc_now: float32 [8, 64, 512], P(None, ('sub', 'grp')), may hold values from -8 to 8
- load_next: float32 [8, 64, 512], P(None, ('sub', 'grp')), may hold values from -10 to 10
- basis_rows: float32 [32768, 256], P(('sub', 'grp')), may hold values from -0.03125 to 0.03125
- piece_owner: int32 [32], replicated, may hold values from 0 to 31, each once
Outputs:
- disp_new: float32 [8, 64, 512], P(None, ('sub', 'grp'))
- vel_new: float32 [8, 64, 512], P(None, ('sub', 'grp'))
- projection: float32 [256, 8], replicated
- r_factor: float32 [8, 8], replicated
- new_columns: float32 [8, 32768], P(None, ('sub', 'grp'))
Inputs may be any that keep to these rules, and one draw needn't show every extreme that they name: piece_owner is a permutation. `rr_inverse`: each of the 64 blocks is symmetric positive definite. `coarse_inverse`: symmetric positive definite.
All inputs are finite; a program needn't handle non-finite values.
Results may differ from a plain program's by a relative error of at most 0.00018.
Values sent between devices are 32-bit elements; how exact they have to be, the bound alone decides.
A program may use at most 64 MiB of HBM per device.

v0:
```python
import math
import jax
import jax.numpy as jnp
from jax import lax
from jax.sharding import PartitionSpec as P

NC = 32
ITERS = 2
NI = 128
highest = lax.Precision.HIGHEST
time_step = 0.5
newmark_beta = 0.25
newmark_gamma = 0.5


def shifted(array, axis, by):
    count = lax.axis_size(axis)
    return lax.ppermute(array, axis, [(i, (i + by) % count) for i in range(count)])


def contract(segment, matrix_rows):
    return lax.dot_general(segment, matrix_rows, (((1,), (1,)), ((), ())), precision=highest)


def shards(
    rr_inverse,
    corner_modes,
    coarse_inverse,
    inertia,
    disp_now,
    vel_now,
    acc_now,
    load_next,
    basis_rows,
    piece_owner,
):
    case_count, sub_count, unknowns = disp_now.shape
    coarse_total = coarse_inverse.shape[1]
    row_count = sub_count * NC
    shifted_rows = jnp.roll(coarse_inverse, NC, axis=1)
    coarse_pairs = jnp.concatenate(
        [
            shifted_rows.reshape(row_count, coarse_total // NC, NC),
            coarse_inverse.reshape(row_count, coarse_total // NC, NC),
        ],
        axis=2,
    ).reshape(row_count, 2 * coarse_total)

    def apply_green(field):
        local_part = jnp.einsum("jab,cjb->cja", rr_inverse, field, precision=highest)
        corner_terms = jnp.einsum("jmb,cjb->cjm", corner_modes, field, precision=highest)
        flat_terms = corner_terms.reshape(case_count, sub_count * 2 * NC)
        owned_sums = contract(
            lax.all_gather(flat_terms, ("sub", "grp"), axis=1, tiled=True), coarse_pairs
        )
        previous = shifted(owned_sums[:, row_count - NC :], ("sub", "grp"), 1)
        owned_blocks = owned_sums.reshape(case_count, sub_count, NC)
        left_values = jnp.concatenate(
            [previous.reshape(case_count, 1, NC), owned_blocks[:, :-1]], axis=1
        )
        coarse_values = jnp.concatenate([left_values, owned_blocks], axis=2)
        return local_part + jnp.einsum(
            "jmb,cjm->cjb", corner_modes, coarse_values, precision=highest
        )

    def interface_jump(field):
        following = shifted(field[:, :1, :NI], ("sub", "grp"), -1)
        first_parts = jnp.concatenate([field[:, 1:, :NI], following], axis=1)
        return field[:, :, unknowns - NI :] - first_parts

    def squared_norm(values):
        return lax.psum(jnp.sum(values * values, axis=(1, 2)), ("sub", "grp"))

    right_side = load_next + inertia[None] * (
        disp_now + time_step * vel_now + (0.5 - newmark_beta) * time_step * time_step * acc_now
    )
    green_rhs = apply_green(right_side)
    residual = interface_jump(green_rhs)
    carried = green_rhs
    direction = residual
    norm_now = squared_norm(residual)
    for iteration in range(ITERS):
        earlier = shifted(direction[:, -1:], ("sub", "grp"), 1)
        left_parts = jnp.concatenate([earlier, direction[:, :-1]], axis=1)
        middle = jnp.zeros((case_count, sub_count, unknowns - 2 * NI), jnp.float32)
        image_field = apply_green(jnp.concatenate([-left_parts, middle, direction], axis=2))
        image = interface_jump(image_field)
        curvature = lax.psum(jnp.sum(direction * image, axis=(1, 2)), ("sub", "grp"))
        alpha = (norm_now / curvature)[:, None, None]
        carried = carried - alpha * image_field
        residual = residual - alpha * image
        if iteration + 1 < ITERS:
            norm_next = squared_norm(residual)
            direction = residual + (norm_next / norm_now)[:, None, None] * direction
            norm_now = norm_next
    accel_new = (
        (carried - disp_now) / (newmark_beta * time_step * time_step)
        - vel_now / (newmark_beta * time_step)
        - (0.5 / newmark_beta - 1.0) * acc_now
    )
    vel_new = vel_now + time_step * ((1.0 - newmark_gamma) * acc_now + newmark_gamma * accel_new)
    piece_total = lax.axis_size(("sub", "grp"))
    piece_rows = unknowns // piece_total
    inverse = (
        jnp.zeros((piece_total,), jnp.int32)
        .at[piece_owner]
        .set(jnp.arange(piece_total, dtype=jnp.int32))
    )
    outgoing = carried.reshape(case_count, sub_count, piece_total, piece_rows)[:, :, inverse, :]
    outgoing = jnp.transpose(outgoing, (0, 2, 1, 3)).reshape(
        case_count, piece_total * sub_count * piece_rows
    )
    received = lax.all_to_all(outgoing, ("sub", "grp"), split_axis=1, concat_axis=1, tiled=True)
    projection_part = lax.dot_general(
        basis_rows, received, (((0,), (1,)), ((), ())), precision=highest
    )
    projection = lax.psum(projection_part, ("sub", "grp"))
    remainder = received - lax.dot_general(
        projection, basis_rows, (((0,), (1,)), ((), ())), precision=highest
    )
    gram_local = lax.dot_general(remainder, remainder, (((1,), (1,)), ((), ())), precision=highest)
    lower = jnp.linalg.cholesky(lax.psum(gram_local, ("sub", "grp")))
    scale_rows = math.sqrt(received.shape[1] * piece_total)
    new_columns = jax.scipy.linalg.solve_triangular(lower, remainder, lower=True) * scale_rows
    r_factor = lower.T / scale_rows
    return (carried, vel_new, projection, r_factor, new_columns)


def solution(mesh):
    return jax.shard_map(
        shards,
        mesh=mesh,
        in_specs=(
            P(("sub", "grp"), None, None),
            P(("sub", "grp"), None, None),
            P(("sub", "grp"), None),
            P(("sub", "grp"), None),
            P(None, ("sub", "grp"), None),
            P(None, ("sub", "grp"), None),
            P(None, ("sub", "grp"), None),
            P(None, ("sub", "grp"), None),
            P(("sub", "grp"), None),
            P(),
        ),
        out_specs=(
            P(None, ("sub", "grp"), None),
            P(None, ("sub", "grp"), None),
            P(),
            P(),
            P(None, ("sub", "grp")),
        ),
        check_vma=False,
    )
```

profile of v0, /device:TPU:0, one launch (start us, length us, event | category | flops | bytes accessed | tf_op | source)
XLA Modules:
  0.0 396.2 jit_solution(17063526511338648422)
XLA Ops:
  0.7 1.5 copy.65
  3.8 43.6 %all_gather.9 = f32[8,4096]{1,0:T(8,128)S(1)} all-gather(f32[8,128]{1,0:T(8,128)S(1)} %reshape.67), channel_id=1, replica_groups=mesh['sub'=8,'grp'=4] {'sub','grp'}, dimensions={1}, use_global_device_ids=true | all-gather | bytes 135168 | tf_op jit(solution)/shard_map/all_gather | solution.py:54
  51.8 1.8 fusion.10
  53.7 4.4 %collective-permute-done = f32[8,32]{1,0:T(8,128)S(1)} collective-permute-done((f32[8,32]{1,0:T(8,128)S(1)}, f32[8,32]{1,0:T(8,128)S(1)}, u32[]{:S(2)}, u32[]{:S(2)}) %collective-permute-start) | collective-permute-done | bytes 1056 | tf_op jit(solution)/shard_map/ppermute | solution.py:18
  60.4 6.6 %collective-permute-done.2 = f32[8,1,128]{2,0,1:T(8,128)S(1)} collective-permute-done((f32[8,1,128]{2,0,1:T(8,128)S(1)}, f32[8,1,128]{2,0,1:T(8,128)S(1)}, u32[]{:S(2)}, u32[]{:S(2)}) %collective-permute-start.2) | collective-permute-done | bytes 4128 | tf_op jit(solution)/shard_map/ppermute | solution.py:18
  67.4 36.7 %all_gather.10 = f32[8,4096]{1,0:T(8,128)S(1)} all-gather(f32[8,128]{1,0:T(8,128)S(1)} %reshape.73), channel_id=1, replica_groups=mesh['sub'=8,'grp'=4] {'sub','grp'}, dimensions={1}, use_global_device_ids=true | all-gather | bytes 135168 | tf_op jit(solution)/shard_map/all_gather | solution.py:54
  104.1 2.7 fusion.50
  107.2 1.8 fusion.5
  109.1 4.4 %collective-permute-done.3 = f32[8,32]{1,0:T(8,128)S(1)} collective-permute-done((f32[8,32]{1,0:T(8,128)S(1)}, f32[8,32]{1,0:T(8,128)S(1)}, u32[]{:S(2)}, u32[]{:S(2)}) %collective-permute-start.3) | collective-permute-done | bytes 1056 | tf_op jit(solution)/shard_map/ppermute | solution.py:18
  116.0 38.1 %all-reduce = (f32[8]{0:T(128)S(1)}, f32[8]{0:T(128)S(1)}) all-reduce(f32[8]{0:T(128)S(1)} %get-tuple-element.21, f32[8]{0:T(128)S(1)} %get-tuple-element.20), channel_id=1, replica_groups=mesh['sub'=8,'grp'=4] {'sub','grp'}, use_global_device_ids=true, to_apply=%region_1.2 | all-reduce | flops 16 | bytes 128 | tf_op jit(solution)/shard_map/psum | solution.py:72
  154.3 42.1 %psum.44 = f32[8]{0:T(128)S(1)} all-reduce(f32[8]{0:T(128)S(1)} %multiply_reduce_fusion), channel_id=1, replica_groups=mesh['sub'=8,'grp'=4] {'sub','grp'}, use_global_device_ids=true, to_apply=%region_5.6 | all-reduce | flops 8 | bytes 64 | tf_op jit(solution)/shard_map/psum | solution.py:72
  197.2 5.9 %collective-permute-done.5 = f32[8,1,128]{2,0,1:T(8,128)S(1)} collective-permute-done((f32[8,1,128]{2,0,1:T(8,128)S(1)}, f32[8,1,128]{2,0,1:T(8,128)S(1)}, u32[]{:S(2)}, u32[]{:S(2)}) %collective-permute-start.5) | collective-permute-done | bytes 4128 | tf_op jit(solution)/shard_map/ppermute | solution.py:18
  203.5 36.7 %all_gather.11 = f32[8,4096]{1,0:T(8,128)S(1)} all-gather(f32[8,128]{1,0:T(8,128)S(1)} %reshape.76), channel_id=1, replica_groups=mesh['sub'=8,'grp'=4] {'sub','grp'}, dimensions={1}, use_global_device_ids=true | all-gather | bytes 135168 | tf_op jit(solution)/shard_map/all_gather | solution.py:54
  240.2 2.7 fusion.51
  243.4 2.5 fusion.6
  246.0 3.7 collective-permute-done.6
  253.6 38.1 %psum.45 = f32[8]{0:T(128)S(1)} all-reduce(f32[8]{0:T(128)S(1)} %fusion.17), channel_id=1, replica_groups=mesh['sub'=8,'grp'=4] {'sub','grp'}, use_global_device_ids=true, to_apply=%region_7.8 | all-reduce | flops 8 | bytes 64 | tf_op jit(solution)/shard_map/psum | solution.py:88
  291.7 1.5 fusion.4
  294.2 1.5 gather_fusion
  296.7 6.5 %all-to-all-start = ((f32[32,1,256]{2,1,0:T(1,128)}), f32[32,1,256]{2,1,0:T(1,128)S(1)}, u32[]{:S(2)}, u32[]{:S(2)}) async-start(f32[32,1,256]{2,1,0:T(1,128)} %reshape.100), calls=%async_computation | async-start | bytes 65536 | tf_op jit(solution)/shard_map/all_to_all | solution.py:113
  303.2 1.4 copy.88
  306.0 4.5 %all-to-all-done = f32[32,1,256]{2,1,0:T(1,128)S(1)} async-done(((f32[32,1,256]{2,1,0:T(1,128)}), f32[32,1,256]{2,1,0:T(1,128)S(1)}, u32[]{:S(2)}, u32[]{:S(2)}) %all-to-all-start) | async-done | bytes 32800 | tf_op jit(solution)/shard_map/all_to_all | solution.py:113
  312.5 38.3 %psum.46 = f32[256,8]{0,1:T(8,128)S(1)} all-reduce(f32[256,8]{0,1:T(8,128)S(1)} %convolution_bitcast_fusion), channel_id=1, replica_groups=mesh['sub'=8,'grp'=4] {'sub','grp'}, use_global_device_ids=true, to_apply=%region_9.10 | all-reduce | flops 2048 | bytes 16384 | tf_op jit(solution)/shard_map/psum | solution.py:117
  351.8 40.1 %psum.47 = f32[8,8]{0,1:T(8,128)S(1)} all-reduce(f32[8,8]{0,1:T(8,128)S(1)} %fusion.52), channel_id=1, replica_groups=mesh['sub'=8,'grp'=4] {'sub','grp'}, use_global_device_ids=true, to_apply=%region_10.11 | all-reduce | flops 64 | bytes 512 | tf_op jit(solution)/shard_map/psum | solution.py:122
  (110 shorter events, 28.4 us)
Async XLA Ops:
  0.6 51.1 %copy-start = (f32[2,512,512]{2,1,0:T(8,128)S(1)}, f32[2,512,512]{2,1,0:T(8,128)}, u32[]{:S(2)}) copy-start(f32[2,512,512]{2,1,0:T(8,128)} %param.10) | copy-start | bytes 6291460
  0.6 2.7 copy-start.6
  0.7 2.7 copy-start.7
  0.7 2.6 copy-start.5
  0.7 2.7 copy-start.2
  2.2 1.1 copy-start.9
  2.2 1.1 copy-start.10
  48.9 1.4 copy-start.1
  51.4 6.7 %collective-permute-start = (f32[8,32]{1,0:T(8,128)S(1)}, f32[8,32]{1,0:T(8,128)S(1)}, u32[]{:S(2)}, u32[]{:S(2)}) collective-permute-start(f32[8,32]{1,0:T(8,128)S(1)} %slice.79), channel_id=1, source_target_pairs={{0,1},{1,2},{2,3},{3,4},{4,5},{5,6},{6,7},{7,8},{8,9},{9,10},{10,1... | collective-permute-start | bytes 3080 | tf_op jit(solution)/shard_map/ppermute | solution.py:18
  58.4 2.0 collective-permute-start.1
  60.4 6.6 %collective-permute-start.2 = (f32[8,1,128]{2,0,1:T(8,128)S(1)}, f32[8,1,128]{2,0,1:T(8,128)S(1)}, u32[]{:S(2)}, u32[]{:S(2)}) collective-permute-start(f32[8,1,128]{2,0,1:T(8,128)S(1)} %get-tuple-element.34), channel_id=1, source_target_pairs={{0,1},{1,2},{2,3},{3,4},{4,5},{5,6},{6,7},{7,8},{8,9},{9,10},{10,1... | collective-permute-start | bytes 12296 | tf_op jit(solution)/shard_map/ppermute | solution.py:18
  104.1 92.4 %copy-start.11 = (s32[32]{0:T(128)S(1)}, s32[32]{0:T(128)}, u32[]{:S(2)}) copy-start(s32[32]{0:T(128)} %param.19) | copy-start | bytes 388
  106.9 6.6 %collective-permute-start.3 = (f32[8,32]{1,0:T(8,128)S(1)}, f32[8,32]{1,0:T(8,128)S(1)}, u32[]{:S(2)}, u32[]{:S(2)}) collective-permute-start(f32[8,32]{1,0:T(8,128)S(1)} %slice.86), channel_id=1, source_target_pairs={{0,1},{1,2},{2,3},{3,4},{4,5},{5,6},{6,7},{7,8},{8,9},{9,10},{10,1... | collective-permute-start | bytes 3080 | tf_op jit(solution)/shard_map/ppermute | solution.py:18
  113.8 2.0 collective-permute-start.4
  196.4 6.6 %collective-permute-start.5 = (f32[8,1,128]{2,0,1:T(8,128)S(1)}, f32[8,1,128]{2,0,1:T(8,128)S(1)}, u32[]{:S(2)}, u32[]{:S(2)}) collective-permute-start(f32[8,1,128]{2,0,1:T(8,128)S(1)} %get-tuple-element.32), channel_id=1, source_target_pairs={{0,1},{1,2},{2,3},{3,4},{4,5},{5,6},{6,7},{7,8},{8,9},{9,10},{10,1... | collective-permute-start | bytes 12296 | tf_op jit(solution)/shard_map/ppermute | solution.py:18
  242.9 6.8 %collective-permute-start.6 = (f32[8,32]{1,0:T(8,128)S(1)}, f32[8,32]{1,0:T(8,128)S(1)}, u32[]{:S(2)}, u32[]{:S(2)}) collective-permute-start(f32[8,32]{1,0:T(8,128)S(1)} %slice.93), channel_id=1, source_target_pairs={{0,1},{1,2},{2,3},{3,4},{4,5},{5,6},{6,7},{7,8},{8,9},{9,10},{10,1... | collective-permute-start | bytes 3080 | tf_op jit(solution)/shard_map/ppermute | solution.py:18
  245.9 66.0 %copy-start.3 = (f32[1024,256]{1,0:T(8,128)S(1)}, f32[1024,256]{1,0:T(8,128)}, u32[]{:S(2)}) copy-start(f32[1024,256]{1,0:T(8,128)} %param.18) | copy-start | bytes 3145732
  250.8 2.7 collective-permute-start.7
  293.2 2.5 copy-start.4
  296.7 13.7 %all-to-all-start = ((f32[32,1,256]{2,1,0:T(1,128)}), f32[32,1,256]{2,1,0:T(1,128)S(1)}, u32[]{:S(2)}, u32[]{:S(2)}) async-start(f32[32,1,256]{2,1,0:T(1,128)} %reshape.100), calls=%async_computation | async-start | bytes 65536 | tf_op jit(solution)/shard_map/all_to_all | solution.py:113
  350.7 45.5 %copy-start.8 = (f32[256,8]{0,1:T(8,128)}, f32[256,8]{0,1:T(8,128)S(1)}, u32[]{:S(2)}) copy-start(f32[256,8]{0,1:T(8,128)S(1)} %psum.46) | copy-start | bytes 24580
where the time goes:
time: 397 us; the launch traced here: 396 us
  blocking collectives  314 us (79%)
  waiting for transfers between devices  33.4 us (8%)
  matrix products  17.6 us (4%)
  local copies, waits for them, and re-layouts  13.2 us (3%)
  starting transfers between devices  10.5 us (3%)
  other arithmetic  6.97 us (2%)
    all_gather x3, blocking collectives, apply_green(): lax.all_gather(flat_terms, ('sub', 'grp'), axis=1, tiled=True)  117 us
    psum x2, blocking collectives, squared_norm(): return lax.psum(jnp.sum(values * values, axis=(1, 2)), ('sub', 'grp'))  80.2 us
    psum x1, blocking collectives, shards(): lower = jnp.linalg.cholesky(lax.psum(gram_local, ('sub', 'grp')))  40.1 us
    psum x1, blocking collectives, shards(): projection = lax.psum(projection_part, ('sub', 'grp'))  38.3 us
    psum x1, blocking collectives, shards(): lax.psum(jnp.sum(direction * image, axis=(1, 2)), ('sub', 'grp'))  38.1 us
    ppermute x8, waiting for transfers between devices, shifted(): lax.ppermute(array, axis, [(i, (i + by) % count) for i in range(count)])  29 us
  transfers between devices with their start and end apart: 9, of which 9 were waited for; matrix products, arithmetic and copies ran while one was open for 2% of the time, Pallas kernels for 0%

commit v1 on v0

--- a/solution.py
+++ b/solution.py
@@ -1,3 +1,4 @@
+import functools
 import math
 import jax
 import jax.numpy as jnp
@@ -11,6 +12,13 @@
 time_step = 0.5
 newmark_beta = 0.25
 newmark_gamma = 0.5
+
+
+def spots_set(x_local, axis_name):
+    return jnp.concatenate(lax.all_gather(x_local, axis_name), axis=1)
+
+
+report_the_kinds = functools.partial(spots_set, axis_name=("sub", "grp"))
 
 
 def shifted(array, axis, by):
@@ -50,9 +58,7 @@
         local_part = jnp.einsum("jab,cjb->cja", rr_inverse, field, precision=highest)
         corner_terms = jnp.einsum("jmb,cjb->cjm", corner_modes, field, precision=highest)
         flat_terms = corner_terms.reshape(case_count, sub_count * 2 * NC)
-        owned_sums = contract(
-            lax.all_gather(flat_terms, ("sub", "grp"), axis=1, tiled=True), coarse_pairs
-        )
+        owned_sums = contract(report_the_kinds(flat_terms), coarse_pairs)
         previous = shifted(owned_sums[:, row_count - NC :], ("sub", "grp"), 1)
         owned_blocks = owned_sums.reshape(case_count, sub_count, NC)
         left_values = jnp.concatenate(

time: 397 us -> 397 us (level)
  no operation moved by 1% of the time
where the time goes in v1:
time: 397 us; the launch traced here: 396 us
  blocking collectives  314 us (79%)
  waiting for transfers between devices  33.4 us (8%)
  matrix products  17.6 us (4%)
  local copies, waits for them, and re-layouts  13.2 us (3%)
  starting transfers between devices  10.5 us (3%)
  other arithmetic  6.97 us (2%)
    all_gather x3, blocking collectives, spots_set(): return jnp.concatenate(lax.all_gather(x_local, axis_name), axis=1)  117 us
    psum x2, blocking collectives, squared_norm(): return lax.psum(jnp.sum(values * values, axis=(1, 2)), ('sub', 'grp'))  80.2 us
    psum x1, blocking collectives, shards(): lower = jnp.linalg.cholesky(lax.psum(gram_local, ('sub', 'grp')))  40.1 us
    psum x1, blocking collectives, shards(): projection = lax.psum(projection_part, ('sub', 'grp'))  38.3 us
    psum x1, blocking collectives, shards(): lax.psum(jnp.sum(direction * image, axis=(1, 2)), ('sub', 'grp'))  38.1 us
    ppermute x8, waiting for transfers between devices, shifted(): lax.ppermute(array, axis, [(i, (i + by) % count) for i in range(count)])  29 us
  transfers between devices with their start and end apart: 9, of which 9 were waited for; matrix products, arithmetic and copies ran while one was open for 2% of the time, Pallas kernels for 0%

profile of v1, /device:TPU:0, one launch (start us, length us, event | category | flops | bytes accessed | tf_op | source)
XLA Modules:
  0.0 396.2 jit_solution(15051737813497982045)
XLA Ops:
  0.7 1.5 copy.65
  3.8 43.6 %all_gather.9 = f32[32,8,128]{2,1,0:T(8,128)S(1)} all-gather(f32[1,8,128]{2,1,0:T(8,128)S(1)} %all_gather_reshape.9), channel_id=1, replica_groups=mesh['sub'=8,'grp'=4] {'sub','grp'}, dimensions={0}, use_global_device_ids=true | all-gather | bytes 135168 | tf_op jit(solution)/shard_map/all_gather | solution.py:18
  51.8 1.8 fusion.16
  53.7 4.4 %collective-permute-done = f32[8,32]{1,0:T(8,128)S(1)} collective-permute-done((f32[8,32]{1,0:T(8,128)S(1)}, f32[8,32]{1,0:T(8,128)S(1)}, u32[]{:S(2)}, u32[]{:S(2)}) %collective-permute-start) | collective-permute-done | bytes 1056 | tf_op jit(solution)/shard_map/ppermute | solution.py:26
  60.4 6.6 %collective-permute-done.2 = f32[8,1,128]{2,0,1:T(8,128)S(1)} collective-permute-done((f32[8,1,128]{2,0,1:T(8,128)S(1)}, f32[8,1,128]{2,0,1:T(8,128)S(1)}, u32[]{:S(2)}, u32[]{:S(2)}) %collective-permute-start.2) | collective-permute-done | bytes 4128 | tf_op jit(solution)/shard_map/ppermute | solution.py:26
  67.4 36.7 %all_gather.10 = f32[32,8,128]{2,1,0:T(8,128)S(1)} all-gather(f32[1,8,128]{2,1,0:T(8,128)S(1)} %all_gather_reshape.10), channel_id=1, replica_groups=mesh['sub'=8,'grp'=4] {'sub','grp'}, dimensions={0}, use_global_device_ids=true | all-gather | bytes 135168 | tf_op jit(solution)/shard_map/all_gather | solution.py:18
  104.1 2.7 fusion.5
  107.2 1.8 fusion.11
  109.1 4.4 %collective-permute-done.3 = f32[8,32]{1,0:T(8,128)S(1)} collective-permute-done((f32[8,32]{1,0:T(8,128)S(1)}, f32[8,32]{1,0:T(8,128)S(1)}, u32[]{:S(2)}, u32[]{:S(2)}) %collective-permute-start.3) | collective-permute-done | bytes 1056 | tf_op jit(solution)/shard_map/ppermute | solution.py:26
  116.0 38.1 %all-reduce = (f32[8]{0:T(128)S(1)}, f32[8]{0:T(128)S(1)}) all-reduce(f32[8]{0:T(128)S(1)} %get-tuple-element.21, f32[8]{0:T(128)S(1)} %get-tuple-element.20), channel_id=1, replica_groups=mesh['sub'=8,'grp'=4] {'sub','grp'}, use_global_device_ids=true, to_apply=%region_1.2 | all-reduce | flops 16 | bytes 128 | tf_op jit(solution)/shard_map/psum | solution.py:78
  154.3 42.1 %psum.44 = f32[8]{0:T(128)S(1)} all-reduce(f32[8]{0:T(128)S(1)} %multiply_reduce_fusion), channel_id=1, replica_groups=mesh['sub'=8,'grp'=4] {'sub','grp'}, use_global_device_ids=true, to_apply=%region_5.6 | all-reduce | flops 8 | bytes 64 | tf_op jit(solution)/shard_map/psum | solution.py:78
  197.2 5.9 %collective-permute-done.5 = f32[8,1,128]{2,0,1:T(8,128)S(1)} collective-permute-done((f32[8,1,128]{2,0,1:T(8,128)S(1)}, f32[8,1,128]{2,0,1:T(8,128)S(1)}, u32[]{:S(2)}, u32[]{:S(2)}) %collective-permute-start.5) | collective-permute-done | bytes 4128 | tf_op jit(solution)/shard_map/ppermute | solution.py:26
  203.5 36.7 %all_gather.11 = f32[32,8,128]{2,1,0:T(8,128)S(1)} all-gather(f32[1,8,128]{2,1,0:T(8,128)S(1)} %all_gather_reshape.11), channel_id=1, replica_groups=mesh['sub'=8,'grp'=4] {'sub','grp'}, dimensions={0}, use_global_device_ids=true | all-gather | bytes 135168 | tf_op jit(solution)/shard_map/all_gather | solution.py:18
  240.2 2.7 fusion.3
  243.4 2.5 fusion.12
  246.0 3.7 collective-permute-done.6
  253.6 38.1 %psum.45 = f32[8]{0:T(128)S(1)} all-reduce(f32[8]{0:T(128)S(1)} %fusion.23), channel_id=1, replica_groups=mesh['sub'=8,'grp'=4] {'sub','grp'}, use_global_device_ids=true, to_apply=%region_7.8 | all-reduce | flops 8 | bytes 64 | tf_op jit(solution)/shard_map/psum | solution.py:94
  291.7 1.5 fusion.10
  294.2 1.5 gather_fusion
  296.7 6.5 %all-to-all-start = ((f32[32,1,256]{2,1,0:T(1,128)}), f32[32,1,256]{2,1,0:T(1,128)S(1)}, u32[]{:S(2)}, u32[]{:S(2)}) async-start(f32[32,1,256]{2,1,0:T(1,128)} %reshape.112), calls=%async_computation | async-start | bytes 65536 | tf_op jit(solution)/shard_map/all_to_all | solution.py:119
  303.2 1.4 copy.88
  306.0 4.5 %all-to-all-done = f32[32,1,256]{2,1,0:T(1,128)S(1)} async-done(((f32[32,1,256]{2,1,0:T(1,128)}), f32[32,1,256]{2,1,0:T(1,128)S(1)}, u32[]{:S(2)}, u32[]{:S(2)}) %all-to-all-start) | async-done | bytes 32800 | tf_op jit(solution)/shard_map/all_to_all | solution.py:119
  312.5 38.3 %psum.46 = f32[256,8]{0,1:T(8,128)S(1)} all-reduce(f32[256,8]{0,1:T(8,128)S(1)} %convolution_bitcast_fusion), channel_id=1, replica_groups=mesh['sub'=8,'grp'=4] {'sub','grp'}, use_global_device_ids=true, to_apply=%region_9.10 | all-reduce | flops 2048 | bytes 16384 | tf_op jit(solution)/shard_map/psum | solution.py:123
  351.8 40.1 %psum.47 = f32[8,8]{0,1:T(8,128)S(1)} all-reduce(f32[8,8]{0,1:T(8,128)S(1)} %fusion.55), channel_id=1, replica_groups=mesh['sub'=8,'grp'=4] {'sub','grp'}, use_global_device_ids=true, to_apply=%region_10.11 | all-reduce | flops 64 | bytes 512 | tf_op jit(solution)/shard_map/psum | solution.py:128
  (110 shorter events, 28.4 us)
Async XLA Ops:
  0.6 51.1 %copy-start = (f32[2,512,512]{2,1,0:T(8,128)S(1)}, f32[2,512,512]{2,1,0:T(8,128)}, u32[]{:S(2)}) copy-start(f32[2,512,512]{2,1,0:T(8,128)} %param.10) | copy-start | bytes 6291460
  0.6 2.7 copy-start.6
  0.7 2.7 copy-start.7
  0.7 2.6 copy-start.5
  0.7 2.7 copy-start.2
  2.2 1.1 copy-start.9
  2.2 1.1 copy-start.10
  48.9 1.4 copy-start.1
  51.4 6.7 %collective-permute-start = (f32[8,32]{1,0:T(8,128)S(1)}, f32[8,32]{1,0:T(8,128)S(1)}, u32[]{:S(2)}, u32[]{:S(2)}) collective-permute-start(f32[8,32]{1,0:T(8,128)S(1)} %slice.79), channel_id=1, source_target_pairs={{0,1},{1,2},{2,3},{3,4},{4,5},{5,6},{6,7},{7,8},{8,9},{9,10},{10,1... | collective-permute-start | bytes 3080 | tf_op jit(solution)/shard_map/ppermute | solution.py:26
  58.4 2.0 collective-permute-start.1
  60.4 6.6 %collective-permute-start.2 = (f32[8,1,128]{2,0,1:T(8,128)S(1)}, f32[8,1,128]{2,0,1:T(8,128)S(1)}, u32[]{:S(2)}, u32[]{:S(2)}) collective-permute-start(f32[8,1,128]{2,0,1:T(8,128)S(1)} %get-tuple-element.34), channel_id=1, source_target_pairs={{0,1},{1,2},{2,3},{3,4},{4,5},{5,6},{6,7},{7,8},{8,9},{9,10},{10,1... | collective-permute-start | bytes 12296 | tf_op jit(solution)/shard_map/ppermute | solution.py:26
  104.1 92.4 %copy-start.11 = (s32[32]{0:T(128)S(1)}, s32[32]{0:T(128)}, u32[]{:S(2)}) copy-start(s32[32]{0:T(128)} %param.19) | copy-start | bytes 388
  106.9 6.6 %collective-permute-start.3 = (f32[8,32]{1,0:T(8,128)S(1)}, f32[8,32]{1,0:T(8,128)S(1)}, u32[]{:S(2)}, u32[]{:S(2)}) collective-permute-start(f32[8,32]{1,0:T(8,128)S(1)} %slice.86), channel_id=1, source_target_pairs={{0,1},{1,2},{2,3},{3,4},{4,5},{5,6},{6,7},{7,8},{8,9},{9,10},{10,1... | collective-permute-start | bytes 3080 | tf_op jit(solution)/shard_map/ppermute | solution.py:26
  113.8 2.0 collective-permute-start.4
  196.4 6.6 %collective-permute-start.5 = (f32[8,1,128]{2,0,1:T(8,128)S(1)}, f32[8,1,128]{2,0,1:T(8,128)S(1)}, u32[]{:S(2)}, u32[]{:S(2)}) collective-permute-start(f32[8,1,128]{2,0,1:T(8,128)S(1)} %get-tuple-element.32), channel_id=1, source_target_pairs={{0,1},{1,2},{2,3},{3,4},{4,5},{5,6},{6,7},{7,8},{8,9},{9,10},{10,1... | collective-permute-start | bytes 12296 | tf_op jit(solution)/shard_map/ppermute | solution.py:26
  242.9 6.8 %collective-permute-start.6 = (f32[8,32]{1,0:T(8,128)S(1)}, f32[8,32]{1,0:T(8,128)S(1)}, u32[]{:S(2)}, u32[]{:S(2)}) collective-permute-start(f32[8,32]{1,0:T(8,128)S(1)} %slice.93), channel_id=1, source_target_pairs={{0,1},{1,2},{2,3},{3,4},{4,5},{5,6},{6,7},{7,8},{8,9},{9,10},{10,1... | collective-permute-start | bytes 3080 | tf_op jit(solution)/shard_map/ppermute | solution.py:26
  245.9 66.0 %copy-start.3 = (f32[1024,256]{1,0:T(8,128)S(1)}, f32[1024,256]{1,0:T(8,128)}, u32[]{:S(2)}) copy-start(f32[1024,256]{1,0:T(8,128)} %param.18) | copy-start | bytes 3145732
  250.8 2.7 collective-permute-start.7
  293.2 2.5 copy-start.4
  296.7 13.7 %all-to-all-start = ((f32[32,1,256]{2,1,0:T(1,128)}), f32[32,1,256]{2,1,0:T(1,128)S(1)}, u32[]{:S(2)}, u32[]{:S(2)}) async-start(f32[32,1,256]{2,1,0:T(1,128)} %reshape.112), calls=%async_computation | async-start | bytes 65536 | tf_op jit(solution)/shard_map/all_to_all | solution.py:119
  350.7 45.5 %copy-start.8 = (f32[256,8]{0,1:T(8,128)}, f32[256,8]{0,1:T(8,128)S(1)}, u32[]{:S(2)}) copy-start(f32[256,8]{0,1:T(8,128)S(1)} %psum.46) | copy-start | bytes 24580
